TPU v7x, 32 devices: a whole 2x2x4 slice. The times are simulated.
32 devices in a mesh: dp: 4 (over y, x), expert: 8 (over z, core).
Axes of the slice: x: 2, y: 2, z: 4, core: 2. Of those that a mesh axis runs over, the one named last changes fastest.
Arguments:
- inputs: bfloat16 [16384, 768], P(('dp', 'expert')), may hold values from -6 to 6
- cotangent: bfloat16 [16384, 768], P(('dp', 'expert')), may hold values from -6 to 6
- lengths: int32 [32], P(('dp', 'expert')), may hold values from 384 to 512, as said below
- routes: int32 [16384, 2], P(('dp', 'expert')), may hold values from 0 to 7, all different within a row; in each aligned block of 512 rows (0 to 511, 512 to 1023, ...) at most 192 rows name the same one
- w_qkv: bfloat16 [768, 2304], P('dp'), may hold values from -0.21875 to 0.21875
- w_attn_out: bfloat16 [768, 768], P('dp'), may hold values from -1.25 to 1.25
- w_router: bfloat16 [768, 8], P('dp'), may hold values from -0.4375 to 0.4375
- gain_attn: bfloat16 [768], P('dp'), may hold values from 0.5 to 1.5
- gain_moe: bfloat16 [768], P('dp'), may hold values from 0.5 to 1.5
- rel_bias: bfloat16 [12, 32], P('dp'), may hold values from -4 to 4
- w_in: bfloat16 [8, 768, 3072], P('expert'), may hold values from -0.21875 to 0.21875
- w_out: bfloat16 [8, 768, 3072], P('expert'), may hold values from -0.109375 to 0.109375
Outputs:
- outputs: bfloat16 [16384, 768], P(('dp', 'expert'))
- d_inputs: bfloat16 [16384, 768], P(('dp', 'expert'))
- grad_qkv: float32 [768, 2304], P('dp')
- grad_attn_out: float32 [768, 768], P('dp')
- grad_router: float32 [768, 8], P('dp')
- grad_gain_attn: float32 [768], P('dp')
- grad_gain_moe: float32 [768], P('dp')
- grad_rel_bias: float32 [12, 32], P('dp')
- grad_w_in: float32 [8, 768, 3072], P('expert', None, 'dp')
- grad_w_out: float32 [8, 768, 3072], P('expert', None, 'dp')
Inputs may be any that keep to these rules, and one draw needn't show every extreme that they name: `lengths`: slots of a sequence at or past its length are padding; some sequence is full and some has the fewest valid tokens. `routes`: a token names two different experts; in the rows of one device no expert is named more than 192 times, a bound that some block reaches.
All inputs are finite; a program needn't handle non-finite values.
Results may differ from a plain program's by a relative error of at most 0.018.
Values may be sent and summed in bfloat16 or wider, within the bound.
A program may use at most 256 MiB of HBM per device.

v0:
```python
import jax
import jax.numpy as jnp
from jax import lax
from jax.sharding import PartitionSpec as P

norm_eps = 1e-06
rel_edges = (19, 21, 24, 27, 31, 35, 40, 46, 52, 59, 67, 77, 87, 99, 113)


def rms_apply(vector, gain_vec):
    return (
        vector * lax.rsqrt(jnp.mean(vector * vector, axis=-1, keepdims=True) + norm_eps) * gain_vec
    )


def bucket_of(distance):
    far_bucket = jnp.full(distance.shape, 16, jnp.int32)
    for edge_value in rel_edges:
        far_bucket = far_bucket + (distance >= edge_value).astype(jnp.int32)
    return jnp.where(distance < 16, distance, far_bucket)


def on_device(
    inputs,
    cotangent,
    lengths,
    routes,
    w_qkv,
    w_attn_out,
    w_router,
    gain_attn,
    gain_moe,
    rel_bias,
    w_in,
    w_out,
):
    w_proj, w_mix, w_gate, gain_one, gain_two, bias_table = (
        lax.all_gather(w_qkv, "dp", axis=0, tiled=True),
        lax.all_gather(w_attn_out, "dp", axis=0, tiled=True),
        lax.all_gather(w_router, "dp", axis=0, tiled=True),
        lax.all_gather(gain_attn, "dp", axis=0, tiled=True),
        lax.all_gather(gain_moe, "dp", axis=0, tiled=True),
        lax.all_gather(rel_bias, "dp", axis=0, tiled=True),
    )
    tok_count, model_width = inputs.shape
    head_count, bucket_count = bias_table.shape
    head_size = model_width // head_count
    top_count = routes.shape[1]
    expert_count = w_gate.shape[1]
    local_count = w_in.shape[0]
    group_count = expert_count // local_count
    capacity = 3 * tok_count * top_count // (2 * expert_count)
    block_rows = min(512, tok_count)
    block_count = tok_count // block_rows
    score_scale = head_size ** (-0.5)
    positions = jnp.arange(tok_count, dtype=jnp.int32)
    valid_mask = (positions < lengths[0]).astype(jnp.float32)
    inputs_wide = inputs.astype(jnp.float32)
    gain_first = gain_one.astype(jnp.float32)
    gain_second = gain_two.astype(jnp.float32)
    normed_attn = rms_apply(inputs_wide, gain_first).astype(jnp.bfloat16)
    proj_qkv = jnp.dot(normed_attn, w_proj, preferred_element_type=jnp.float32).astype(jnp.bfloat16)
    query_heads = proj_qkv[:, :model_width].reshape(tok_count, head_count, head_size)
    key_heads = proj_qkv[:, model_width : 2 * model_width].reshape(tok_count, head_count, head_size)
    value_heads = proj_qkv[:, 2 * model_width :].reshape(tok_count, head_count, head_size)
    bucket_ids = jnp.arange(bucket_count, dtype=jnp.int32)

    def scores_of(row_start):
        distance = (row_start + jnp.arange(block_rows, dtype=jnp.int32))[:, None] - positions[
            None, :
        ]
        allowed = (distance >= 0) & (positions[None, :] < lengths[0])
        one_hot = (bucket_of(jnp.maximum(distance, 0))[:, :, None] == bucket_ids).astype(
            jnp.bfloat16
        )
        bias_term = jnp.einsum(
            "hb,qkb->hqk", bias_table, one_hot, preferred_element_type=jnp.float32
        )
        raw_scores = (
            jnp.einsum("qhd,khd->hqk", query_heads, key_heads, preferred_element_type=jnp.float32)
            * score_scale
            + bias_term
        )
        return (query_heads, one_hot, jnp.where(allowed[None], raw_scores, -1e30))

    def forward_block(block_index):
        row_start = block_index * block_rows
        query_block, one_hot, raw_scores = scores_of(row_start)
        top_score = jnp.max(raw_scores, axis=-1, keepdims=True)
        exp_terms = jnp.exp(raw_scores - top_score)
        row_total = jnp.sum(exp_terms, axis=-1, keepdims=True)
        attn_prob = (exp_terms / row_total).astype(jnp.bfloat16)
        head_out = jnp.einsum(
            "hqk,khd->qhd", attn_prob, value_heads, preferred_element_type=jnp.float32
        )
        return (
            head_out.reshape(block_rows, model_width).astype(jnp.bfloat16),
            top_score[..., 0] + jnp.log(row_total[..., 0]),
        )

    attn_heads, log_totals = lax.map(forward_block, jnp.arange(block_count, dtype=jnp.int32))
    attn_heads = attn_heads.reshape(tok_count, model_width)
    attn_proj = jnp.dot(attn_heads, w_mix, preferred_element_type=jnp.float32)
    hidden = inputs_wide + valid_mask[:, None] * attn_proj
    normed_moe = rms_apply(hidden, gain_second).astype(jnp.bfloat16)
    logits = jnp.dot(normed_moe, w_gate, preferred_element_type=jnp.float32)
    expert_ids = jnp.arange(expert_count, dtype=jnp.int32)
    chosen_mask = (routes[:, :, None] == expert_ids).astype(jnp.float32)
    chosen = jnp.sum(logits[:, None, :] * chosen_mask, axis=-1)
    gate_pair = jax.nn.softmax(chosen, axis=-1)
    gate_used = gate_pair * valid_mask[:, None]
    flat_routes = routes.reshape(-1)
    flat_valid = jnp.broadcast_to(valid_mask[:, None], routes.shape).reshape(-1) > 0
    route_hot = ((flat_routes[:, None] == expert_ids) & flat_valid[:, None]).astype(jnp.int32)
    rank_in = jnp.sum((jnp.cumsum(route_hot, axis=0) - route_hot) * route_hot, axis=1)
    slot_index = jnp.where(flat_valid, flat_routes * capacity + rank_in, expert_count * capacity)
    route_ids = jnp.arange(tok_count * top_count, dtype=jnp.int32)
    source = jnp.zeros((expert_count * capacity + 1,), jnp.int32).at[slot_index].set(route_ids)[:-1]
    filled = jnp.zeros((expert_count * capacity + 1,), jnp.bfloat16).at[slot_index].set(1)[:-1]
    send_rows = (normed_moe[source // top_count] * filled[:, None]).reshape(
        group_count, local_count, capacity, model_width
    )
    recv_rows = lax.all_to_all(send_rows, "expert", split_axis=0, concat_axis=0, tiled=True)
    pre_act = jnp.einsum("nekd,edf->nekf", recv_rows, w_in, preferred_element_type=jnp.float32)
    activation = jax.nn.gelu(pre_act).astype(jnp.bfloat16)
    expert_out = jnp.einsum(
        "nekf,edf->nekd", activation, w_out, preferred_element_type=jnp.float32
    ).astype(jnp.bfloat16)
    returned = lax.all_to_all(expert_out, "expert", split_axis=0, concat_axis=0, tiled=True)
    results = (returned, recv_rows, pre_act)
    returned = results[0]
    kept_rows = results[1]
    out_table = jnp.concatenate(
        [
            returned.reshape(expert_count * capacity, model_width),
            jnp.zeros((1, model_width), jnp.bfloat16),
        ],
        axis=0,
    )
    picked = out_table[slot_index].reshape(tok_count, top_count, model_width).astype(jnp.float32)
    moe_out = jnp.sum(gate_used[:, :, None] * picked, axis=1)
    outputs = (valid_mask[:, None] * (hidden + moe_out)).astype(jnp.bfloat16)
    grad_out = cotangent.astype(jnp.float32) * valid_mask[:, None]
    d_gate = jnp.sum(grad_out[:, None, :] * picked, axis=-1) * valid_mask[:, None]
    d_chosen = gate_pair * (d_gate - jnp.sum(gate_pair * d_gate, axis=-1, keepdims=True))
    d_logits = jnp.sum(d_chosen[:, :, None] * chosen_mask, axis=1).astype(jnp.bfloat16)
    grad_router = jnp.dot(normed_moe.T, d_logits, preferred_element_type=jnp.float32)
    d_normed = jnp.dot(d_logits, w_gate.T, preferred_element_type=jnp.float32)
    route_weight = gate_used.reshape(-1)
    d_send = (
        grad_out[source // top_count] * (route_weight[source] * filled.astype(jnp.float32))[:, None]
    ).astype(jnp.bfloat16)
    d_send = d_send.reshape(group_count, local_count, capacity, model_width)
    d_recv = lax.all_to_all(d_send, "expert", split_axis=0, concat_axis=0, tiled=True)
    pre_act = results[2]
    act_full, gelu_back = jax.vjp(jax.nn.gelu, pre_act)
    activation = act_full.astype(jnp.bfloat16)
    d_act = jnp.einsum("nekd,edf->nekf", d_recv, w_out, preferred_element_type=jnp.float32)
    d_pre = gelu_back(d_act)[0].astype(jnp.bfloat16)
    full_w_out = jnp.einsum(
        "nekd,nekf->edf", d_recv, activation, preferred_element_type=jnp.float32
    )
    full_w_in = jnp.einsum("nekd,nekf->edf", kept_rows, d_pre, preferred_element_type=jnp.float32)
    d_rows = jnp.einsum("nekf,edf->nekd", d_pre, w_in, preferred_element_type=jnp.float32).astype(
        jnp.bfloat16
    )
    d_returned = lax.all_to_all(d_rows, "expert", split_axis=0, concat_axis=0, tiled=True)
    grad_w_in, grad_w_out = (
        lax.psum_scatter(
            full_w_in.astype(jnp.bfloat16), "dp", scatter_dimension=2, tiled=True
        ).astype(jnp.float32),
        lax.psum_scatter(
            full_w_out.astype(jnp.bfloat16), "dp", scatter_dimension=2, tiled=True
        ).astype(jnp.float32),
    )
    d_table = jnp.concatenate(
        [
            d_returned.reshape(expert_count * capacity, model_width),
            jnp.zeros((1, model_width), jnp.bfloat16),
        ],
        axis=0,
    )
    d_normed = d_normed + jnp.sum(
        d_table[slot_index].reshape(tok_count, top_count, model_width).astype(jnp.float32), axis=1
    )
    second_val, second_back = jax.vjp(rms_apply, hidden, gain_second)
    d_hidden_norm, grad_gain_moe = second_back(d_normed)
    d_hidden = grad_out + d_hidden_norm
    d_attn_proj = (d_hidden * valid_mask[:, None]).astype(jnp.bfloat16)
    grad_attn_out = jnp.dot(attn_heads.T, d_attn_proj, preferred_element_type=jnp.float32)
    d_heads = (
        jnp.dot(d_attn_proj, w_mix.T, preferred_element_type=jnp.float32)
        .astype(jnp.bfloat16)
        .reshape(tok_count, head_count, head_size)
    )

    def backward_block(carry, block_index):
        d_keys, d_values, d_bias = carry
        row_start = block_index * block_rows
        query_block, one_hot, raw_scores = scores_of(row_start)
        attn_full = jnp.exp(raw_scores - log_totals[block_index][..., None])
        attn_prob = attn_full.astype(jnp.bfloat16)
        d_values = d_values + jnp.einsum(
            "hqk,qhd->khd", attn_prob, d_heads, preferred_element_type=jnp.float32
        )
        d_prob = jnp.einsum(
            "qhd,khd->hqk", d_heads, value_heads, preferred_element_type=jnp.float32
        )
        d_scores = (
            attn_full * (d_prob - jnp.sum(attn_full * d_prob, axis=-1, keepdims=True))
        ).astype(jnp.bfloat16)
        d_query = (
            jnp.einsum("hqk,khd->qhd", d_scores, key_heads, preferred_element_type=jnp.float32)
            * score_scale
        )
        d_keys = (
            d_keys
            + jnp.einsum("hqk,qhd->khd", d_scores, query_block, preferred_element_type=jnp.float32)
            * score_scale
        )
        d_bias = d_bias + jnp.einsum(
            "hqk,qkb->hb", d_scores, one_hot, preferred_element_type=jnp.float32
        )
        return ((d_keys, d_values, d_bias), d_query)

    start_carry = (
        jnp.zeros((tok_count, head_count, head_size), jnp.float32),
        jnp.zeros((tok_count, head_count, head_size), jnp.float32),
        jnp.zeros((head_count, bucket_count), jnp.float32),
    )
    final_carry, d_queries = lax.scan(
        backward_block, start_carry, jnp.arange(block_count, dtype=jnp.int32)
    )
    d_keys, d_values, grad_rel_bias = final_carry
    d_qkv = jnp.concatenate(
        [
            d_queries.reshape(tok_count, model_width),
            d_keys.reshape(tok_count, model_width),
            d_values.reshape(tok_count, model_width),
        ],
        axis=1,
    ).astype(jnp.bfloat16)
    grad_qkv = jnp.dot(normed_attn.T, d_qkv, preferred_element_type=jnp.float32)
    d_normed_attn = jnp.dot(d_qkv, w_proj.T, preferred_element_type=jnp.float32)
    first_val, first_back = jax.vjp(rms_apply, inputs_wide, gain_first)
    d_norm_in, grad_gain_attn = first_back(d_normed_attn)
    d_inputs = (d_hidden + d_norm_in).astype(jnp.bfloat16)
    summed = lax.psum(
        (grad_qkv, grad_attn_out, grad_router, grad_gain_attn, grad_gain_moe, grad_rel_bias),
        "expert",
    )
    shares = (
        lax.psum_scatter(
            summed[0].astype(jnp.bfloat16), "dp", scatter_dimension=0, tiled=True
        ).astype(jnp.float32),
        lax.psum_scatter(
            summed[1].astype(jnp.bfloat16), "dp", scatter_dimension=0, tiled=True
        ).astype(jnp.float32),
        lax.psum_scatter(
            summed[2].astype(jnp.bfloat16), "dp", scatter_dimension=0, tiled=True
        ).astype(jnp.float32),
        lax.psum_scatter(
            summed[3].astype(jnp.bfloat16), "dp", scatter_dimension=0, tiled=True
        ).astype(jnp.float32),
        lax.psum_scatter(
            summed[4].astype(jnp.bfloat16), "dp", scatter_dimension=0, tiled=True
        ).astype(jnp.float32),
        lax.psum_scatter(
            summed[5].astype(jnp.bfloat16), "dp", scatter_dimension=0, tiled=True
        ).astype(jnp.float32),
    )
    return (
        outputs,
        d_inputs,
        shares[0],
        shares[1],
        shares[2],
        shares[3],
        shares[4],
        shares[5],
        grad_w_in,
        grad_w_out,
    )


def solution(mesh):
    placed = (
        P(("dp", "expert"), None),
        P(("dp", "expert"), None),
        P(("dp", "expert")),
        P(("dp", "expert"), None),
        P("dp", None),
        P("dp", None),
        P("dp", None),
        P("dp"),
        P("dp"),
        P("dp", None),
        P("expert", None, None),
        P("expert", None, None),
    )
    return jax.shard_map(
        on_device,
        mesh=mesh,
        in_specs=placed,
        out_specs=(
            P(("dp", "expert"), None),
            P(("dp", "expert"), None),
            P("dp", None),
            P("dp", None),
            P("dp", None),
            P("dp"),
            P("dp"),
            P("dp", None),
            P("expert", None, "dp"),
            P("expert", None, "dp"),
        ),
        check_vma=False,
    )
```

profile of v0, /device:TPU:0, one launch (start us, length us, event | category | flops | bytes accessed | tf_op | source)
XLA Modules:
  0.0 836.9 jit_solution(11482958832264062407)
XLA Ops:
  14.5 11.6 %all-reduce.9 = (bf16[768]{0:T(1024)(128)(2,1)S(1)}, bf16[768]{0:T(1024)(128)(2,1)S(1)}) all-reduce(bf16[768]{0:T(1024)(128)(2,1)S(1)} %dynamic-update-slice, bf16[768]{0:T(1024)(128)(2,1)S(1)} %dynamic-update-slice.1), channel_id=1, replica_groups=mesh['dp'=4,'expert'=8] {'dp'}, use_global_device_ids=true, to_apply=%add.2 | all-reduce | flops 1536 | bytes 6144
  26.0 7.3 all-gather
  37.0 7.6 scatter_custom_fusion.1
  44.7 4.5 scatter_custom_fusion
  49.2 8.5 %fusion.1 = f32[512,512,12]{0,2,1:T(8,128)} fusion(bf16[12,32,1]{1,0,2:T(8,128)(2,1)S(1)} %reshape.597, s32[512,512]{0,1:T(8,128)S(1)} %compare_select_fusion), kind=kOutput, calls=%fused_computation.9 | convolution fusion | flops 209715200 | bytes 13632256 | tf_op jit(solution)/shard_map/while/body/eval_jaxpr/hb,qkb->hqk/dot_general | solution.py:76
  59.8 4.1 convolution_convert_fusion
  66.9 15.6 %fusion.132 = (f32[12,512]{1,0:T(8,128)S(1)}, f32[12,512,512]{1,2,0:T(8,128)S(1)}) fusion(f32[512,512,12]{0,2,1:T(8,128)} %fusion.1, bf16[512,12,64]{0,2,1:T(8,128)(2,1)S(1)} %bitcast.217, bf16[512,12,64]{0,2,1:T(8,128)(2,1)S(1)} %bitcast.212, pred[512,512]{0,1:T(8,128)(4,1)S(1)} %fusion.93), kind=kOutput, calls=%fused_computation.192 | convolution fusion | flops 415229952 | bytes 27025408 | tf_op jit(solution)/shard_map/while/body/eval_jaxpr/qhd,khd->hqk/dot_general | solution.py:80
  87.4 7.1 fusion.72
  98.5 5.0 gather_fusion
  105.1 4.8 all-to-all-start
  109.9 8.1 all-gather.1
  118.4 5.6 gather_fusion.2
  124.7 5.9 gather_fusion.3
  130.6 4.1 multiply_convert_fusion.1
  134.7 29.9 %all-to-all-done = bf16[8,1,192,768]{3,2,1,0:T(8,128)(2,1)} async-done(((bf16[8,1,192,768]{3,2,1,0:T(8,128)(2,1)}), bf16[8,1,192,768]{3,2,1,0:T(8,128)(2,1)}, u32[]{:S(2)}, u32[]{:S(2)}) %all-to-all-start) | async-done | bytes 2359328 | tf_op jit(solution)/shard_map/all_to_all | solution.py:123
  164.6 4.8 all-to-all-start.2
  169.4 13.7 %fusion.38 = f32[8,192,3072]{2,1,0:T(8,128)} fusion(bf16[1,768,3072]{2,1,0:T(8,128)(2,1)} %param.22, bf16[8,1,192,768]{3,2,1,0:T(8,128)(2,1)} %all-to-all-done), kind=kOutput, calls=%fused_computation.54 | convolution fusion | flops 7247757312 | bytes 25952256 | tf_op jit(solution)/shard_map/nekd,edf->nekf/dot_general | solution.py:124
  183.1 17.4 %convert_bitcast_fusion.1 = bf16[8,1,192,768]{3,2,1,0:T(8,128)(2,1)} fusion(bf16[1,768,3072]{2,1,0:T(8,128)(2,1)} %param.23, f32[8,192,3072]{2,1,0:T(8,128)} %fusion.38), kind=kOutput, calls=%fused_computation.76 | convolution fusion | flops 7291404288 | bytes 25952256 | tf_op jit(solution)/shard_map/nekf,edf->nekd/dot_general | solution.py:126
  200.5 23.6 %all-to-all-done.2 = bf16[8,1,192,768]{3,2,1,0:T(8,128)(2,1)} async-done(((bf16[8,1,192,768]{3,2,1,0:T(8,128)(2,1)}), bf16[8,1,192,768]{3,2,1,0:T(8,128)(2,1)}, u32[]{:S(2)}, u32[]{:S(2)}) %all-to-all-start.2) | async-done | bytes 2359328 | tf_op jit(solution)/shard_map/all_to_all | solution.py:154
  224.1 4.5 all-to-all-start.1
  228.6 22.0 %fusion.8 = bf16[8,1,192,3072]{3,2,0,1:T(8,128)(2,1)S(1)} fusion(f32[8,192,3072]{2,1,0:T(8,128)} %fusion.38, bf16[1,768,3072]{2,1,0:T(8,128)(2,1)} %param.23, bf16[8,1,192,768]{3,2,1,0:T(8,128)(2,1)} %all-to-all-done.2), kind=kOutput, calls=%fused_computation.18 | convolution fusion | flops 7342129152 | bytes 35389440 | tf_op jit(solution)/shard_map/nekd,edf->nekf/dot_general | solution.py:158
  250.7 3.6 copy-done.38
  254.3 11.1 %convert_bitcast_fusion = bf16[8,1,192,768]{3,2,1,0:T(8,128)(2,1)} fusion(bf16[1,768,3072]{2,1,0:T(8,128)(2,1)} %param.22, bf16[8,1,192,3072]{3,2,0,1:T(8,128)(2,1)S(1)} %fusion.8), kind=kOutput, calls=%fused_computation.75 | convolution fusion | flops 7248936960 | bytes 16515072 | tf_op jit(solution)/shard_map/nekf,edf->nekd/dot_general | solution.py:164
  265.4 17.9 %all-to-all-done.1 = bf16[8,1,192,768]{3,2,1,0:T(8,128)(2,1)} async-done(((bf16[8,1,192,768]{3,2,1,0:T(8,128)(2,1)}), bf16[8,1,192,768]{3,2,1,0:T(8,128)(2,1)}, u32[]{:S(2)}, u32[]{:S(2)}) %all-to-all-start.1) | async-done | bytes 2359328 | tf_op jit(solution)/shard_map/all_to_all | solution.py:129
  283.3 4.4 all-to-all-start.3
  287.8 3.3 concatenate.10
  291.0 7.7 gather_fusion.1
  298.8 4.9 reshape.522
  303.7 9.4 %multiply_reduce_fusion.1 = (f32[512,2]{1,0:T(8,128)S(1)}, f32[512,768]{1,0:T(8,128)}) fusion(f32[512,2,768]{2,1,0:T(2,128)} %reshape.522, f32[512,768]{1,0:T(8,128)S(1)} %convert_multiply_fusion.4, f32[512,2]{1,0:T(8,128)S(1)} %copy.127), kind=kLoop, calls=%fused_computation.60 | loop fusion | flops 2751488 | bytes 6299648 | tf_op jit(solution)/shard_map/reduce_sum | solution.py:144
  313.4 28.9 %all-to-all-done.3 = bf16[8,1,192,768]{3,2,1,0:T(8,128)(2,1)} async-done(((bf16[8,1,192,768]{3,2,1,0:T(8,128)(2,1)}), bf16[8,1,192,768]{3,2,1,0:T(8,128)(2,1)}, u32[]{:S(2)}, u32[]{:S(2)}) %all-to-all-start.3) | async-done | bytes 2359328 | tf_op jit(solution)/shard_map/all_to_all | solution.py:167
  344.2 5.2 gather_fusion.4
  349.4 5.2 reshape.523
  354.6 5.7 reduce_sum.183
  367.8 7.7 fusion.69
  375.4 7.7 multiply_reduce_fusion
  383.2 5.3 multiply_convert_fusion
  388.5 10.4 %fusion.73 = f32[12,32]{1,0:T(8,128)S(1)} fusion(s32[512,512]{0,1:T(8,128)} %copy-done.12, bf16[12,512,512]{1,2,0:T(8,128)(2,1)} %multiply_convert_fusion), kind=kOutput, calls=%fused_computation.100 | convolution fusion | flops 209715200 | bytes 7341568 | tf_op jit(solution)/shard_map/while/body/eval_jaxpr/hqk,qkb->hb/dot_general | solution.py:221
  398.9 4.9 multiply_convert_fusion.2
  405.2 5.2 fusion.94
  410.4 3.6 fusion.63
  414.0 188.6 %all-reduce.11 = (bf16[768,2304]{1,0:T(8,128)(2,1)}, bf16[768,768]{1,0:T(8,128)(2,1)}, bf16[768,8]{0,1:T(8,128)(2,1)S(1)}, bf16[768]{0:T(1024)(128)(2,1)S(1)}, b...) all-reduce(f32[768,2304]{1,0:T(8,128)} %fusion.94, ...), channel_id=1, replica_groups=mesh['dp'=4,'expert'=8] {'expert'}, use_global_device_ids=true, to_apply=%region_20.21 | all-reduce | flops 2367360 | bytes 14204160 | tf_op jit(solution)/shard_map/psum | solution.py:248
  604.1 14.3 %fusion.43 = bf16[1,768,3072]{2,1,0:T(8,128)(2,1)} fusion(f32[8,192,3072]{2,1,0:T(8,128)} %fusion.38, bf16[8,1,192,768]{3,2,1,0:T(8,128)(2,1)} %all-to-all-done.2), kind=kOutput, calls=%fused_computation.58 | convolution fusion | flops 7292583936 | bytes 25952256 | tf_op jit(solution)/shard_map/nekd,nekf->edf/dot_general | solution.py:160
  618.5 12.5 %fusion.40 = bf16[1,768,3072]{2,1,0:T(8,128)(2,1)} fusion(bf16[8,1,192,3072]{3,2,0,1:T(8,128)(2,1)} %copy-done.38, bf16[8,1,192,768]{3,2,1,0:T(8,128)(2,1)} %all-to-all-done), kind=kOutput, calls=%fused_computation.57 | convolution fusion | flops 7250116608 | bytes 16515072 | tf_op jit(solution)/shard_map/nekd,nekf->edf/dot_general | solution.py:163
  633.1 9.6 %all-reduce.8 = (bf16[768]{0:T(1024)(128)(2,1)S(1)}, bf16[768]{0:T(1024)(128)(2,1)S(1)}, bf16[12,32]{1,0:T(8,128)(2,1)S(1)}) all-reduce(bf16[768]{0:T(1024)(128)(2,1)S(1)} %get-tuple-element.77, bf16[768]{0:T(1024)(128)(2,1)S(1)} %get-tuple-element.78, ...), channel_id=5, replica_groups=mesh['dp'=4,'expert'=8] {'dp'}, use_global_device_ids=true, to_apply=%region_28.29.clone | all-reduce | flops 1920 | bytes 7680
  648.8 8.6 %reduce-scatter.10.cloned.1.call-done = bf16[192,768]{1,0:T(8,128)(2,1)} async-done(((bf16[768,768]{1,0:T(8,128)(2,1)}), bf16[192,768]{1,0:T(8,128)(2,1)}) %reduce-scatter.10.cloned.1.call-update) | async-done | bytes 294928 | tf_op jit(solution)/shard_map/reduce_scatter | solution.py:256
  659.2 58.0 %reduce-scatter.14.cloned.1.call-done = bf16[1,768,768]{2,1,0:T(8,128)(2,1)} async-done(((bf16[1,768,3072]{2,1,0:T(8,128)(2,1)}), bf16[1,768,768]{2,1,0:T(8,128)(2,1)}) %reduce-scatter.14.cloned.1.call-update) | async-done | bytes 1179664 | tf_op jit(solution)/shard_map/reduce_scatter | solution.py:172
  720.1 57.0 %reduce-scatter.12.cloned.1.call-done = bf16[1,768,768]{2,1,0:T(8,128)(2,1)} async-done(((bf16[1,768,3072]{2,1,0:T(8,128)(2,1)}), bf16[1,768,768]{2,1,0:T(8,128)(2,1)}) %reduce-scatter.12.cloned.1.call-update) | async-done | bytes 1179664 | tf_op jit(solution)/shard_map/reduce_scatter | solution.py:169
  779.9 47.4 %reduce-scatter.8.cloned.1.call-done = bf16[192,2304]{1,0:T(8,128)(2,1)} async-done(((bf16[768,2304]{1,0:T(8,128)(2,1)}), bf16[192,2304]{1,0:T(8,128)(2,1)}) %reduce-scatter.8.cloned.1.call-update) | async-done | bytes 884752 | tf_op jit(solution)/shard_map/reduce_scatter | solution.py:253
  (190 shorter events, 55.3 us)
Async XLA Ops:
  7.2 5.5 copy-start.32
  7.2 5.2 copy-start.15
  7.2 6.8 copy-start.36
  7.2 7.0 copy-start.37
  7.2 18.8 %copy-start.33 = (bf16[3,32]{1,0:T(4,128)(2,1)S(1)}, bf16[3,32]{1,0:T(4,128)(2,1)}, u32[]{:S(2)}) copy-start(bf16[3,32]{1,0:T(4,128)(2,1)} %param.21) | copy-start | bytes 580
  7.2 52.6 %all-gather.5.cloned.1.call-start = ((), (), s32[]{:S(2)}) async-start(), calls=%async_computation.9 | async-start | bytes 4423680 | tf_op jit(solution)/shard_map/all_gather | solution.py:38
  8.0 86.6 %all-gather.7.cloned.1.call-start = ((), (), s32[]{:S(2)}) async-start(), calls=%async_computation.10 | async-start | bytes 1474560 | tf_op jit(solution)/shard_map/all_gather | solution.py:39
  12.4 45.4 %copy-start.12 = (s32[512,512]{0,1:T(8,128)}, s32[512,512]{0,1:T(8,128)S(1)}, u32[]{:S(2)}) copy-start(s32[512,512]{0,1:T(8,128)S(1)} %compare_select_fusion) | copy-start | bytes 3145732
  12.7 20.7 %copy-start.23 = (f32[512]{0:T(512)}, f32[512]{0:T(512)S(1)}, u32[]{:S(2)}) copy-start(f32[512]{0:T(512)S(1)} %fusion.67) | copy-start | bytes 6148
  12.7 47.1 %copy-start.29 = (f32[512]{0:T(512)}, f32[512]{0:T(512)S(1)}, u32[]{:S(2)}) copy-start(f32[512]{0:T(512)S(1)} %fusion.115) | copy-start | bytes 6148
  26.0 33.8 %copy-start.25 = (f32[768]{0:T(1024)}, f32[768]{0:T(1024)S(1)}, u32[]{:S(2)}) copy-start(f32[768]{0:T(1024)S(1)} %convert_element_type.378) | copy-start | bytes 9220
  37.0 7.7 copy-start.27
  65.2 17.3 %copy-start.6 = (bf16[512,768]{0,1:T(8,128)(2,1)}, bf16[512,768]{0,1:T(8,128)(2,1)S(1)}, u32[]{:S(2)}) copy-start(bf16[512,768]{0,1:T(8,128)(2,1)S(1)} %copy.123) | copy-start | bytes 2359300
  66.9 15.6 %copy-start.10 = (bf16[512,768]{0,1:T(8,128)(2,1)}, bf16[512,768]{0,1:T(8,128)(2,1)S(1)}, u32[]{:S(2)}) copy-start(bf16[512,768]{0,1:T(8,128)(2,1)S(1)} %copy.122) | copy-start | bytes 2359300
  82.5 4.6 copy-start
  87.4 7.1 copy-start.14
  94.5 3.9 copy-start.20
  105.1 4.8 copy-start.31
  105.1 13.0 %copy-start.17 = (bf16[512,768]{1,0:T(8,128)(2,1)S(1)}, bf16[512,768]{1,0:T(8,128)(2,1)}, u32[]{:S(2)}) copy-start(bf16[512,768]{1,0:T(8,128)(2,1)} %param.13) | copy-start | bytes 2359300
  105.1 59.5 %all-to-all-start = ((bf16[8,1,192,768]{3,2,1,0:T(8,128)(2,1)}), bf16[8,1,192,768]{3,2,1,0:T(8,128)(2,1)}, u32[]{:S(2)}, u32[]{:S(2)}) async-start(bf16[8,1,192,768]{3,2,1,0:T(8,128)(2,1)} %broadcast_multiply_fusion), calls=%async_computation | async-start | bytes 4718592 | tf_op jit(solution)/shard_map/all_to_all | solution.py:123
  118.4 5.9 copy-start.22
  164.6 59.5 %all-to-all-start.2 = ((bf16[8,1,192,768]{3,2,1,0:T(8,128)(2,1)}), bf16[8,1,192,768]{3,2,1,0:T(8,128)(2,1)}, u32[]{:S(2)}, u32[]{:S(2)}) async-start(bf16[8,1,192,768]{3,2,1,0:T(8,128)(2,1)} %multiply_convert_fusion.1), calls=%async_computation.2 | async-start | bytes 4718592 | tf_op jit(solution)/shard_map/all_to_all | solution.py:154
  224.1 59.2 %all-to-all-start.1 = ((bf16[8,1,192,768]{3,2,1,0:T(8,128)(2,1)}), bf16[8,1,192,768]{3,2,1,0:T(8,128)(2,1)}, u32[]{:S(2)}, u32[]{:S(2)}) async-start(bf16[8,1,192,768]{3,2,1,0:T(8,128)(2,1)} %convert_bitcast_fusion.1), calls=%async_computation.1 | async-start | bytes 4718592 | tf_op jit(solution)/shard_map/all_to_all | solution.py:129
  250.7 3.7 copy-start.38
  265.4 22.3 %copy-start.28 = (s32[1024,1]{0,1:T(1,128)S(1)}, s32[1024,1]{0,1:T(1,128)}, u32[]{:S(2)}) copy-start(s32[1024,1]{0,1:T(1,128)} %copy-done.27) | copy-start | bytes 12292
  283.3 59.0 %all-to-all-start.3 = ((bf16[8,1,192,768]{3,2,1,0:T(8,128)(2,1)}), bf16[8,1,192,768]{3,2,1,0:T(8,128)(2,1)}, u32[]{:S(2)}, u32[]{:S(2)}) async-start(bf16[8,1,192,768]{3,2,1,0:T(8,128)(2,1)} %convert_bitcast_fusion), calls=%async_computation.3 | async-start | bytes 4718592 | tf_op jit(solution)/shard_map/all_to_all | solution.py:167
  287.7 359.7 %reduce-scatter.16.cloned.1.call-start = ((), (), s32[]{:S(2)}) async-start(), calls=%async_computation.15 | async-start | bytes 245760
  354.6 5.7 copy-start.5
  360.4 1.4 copy-start.13
  360.4 1.6 copy-start.18
  362.0 1.5 copy-start.21
  363.4 2.3 copy-start.2
  363.4 2.3 copy-start.35
  367.8 15.4 %slice-start = ((s8[12582912]{0:T(1024)(128)(4,1)}), s8[4194304]{0:T(1024)(128)(4,1)S(1)}, s32[]{:S(2)}) async-start(s8[12582912]{0:T(1024)(128)(4,1)} %bitcast.209), calls=%async_computation.16 | async-start | bytes 8388608
  367.8 15.4 %slice-start.1 = ((s8[12582912]{0:T(1024)(128)(4,1)}), s8[4194304]{0:T(1024)(128)(4,1)S(1)}, s32[]{:S(2)}) async-start(s8[12582912]{0:T(1024)(128)(4,1)} %bitcast.209), calls=%async_computation.17 | async-start | bytes 8388608
  375.4 7.8 slice-start.2
  388.5 10.4 %copy-start.11 = (bf16[512,768]{0,1:T(8,128)(2,1)S(1)}, bf16[512,768]{0,1:T(8,128)(2,1)}, u32[]{:S(2)}) copy-start(bf16[512,768]{0,1:T(8,128)(2,1)} %copy-done.10) | copy-start | bytes 2359300
  398.9 5.0 copy-start.1
  398.9 5.0 copy-start.7
  403.9 1.4 copy-start.19
  405.2 5.2 copy-start.34
  410.4 3.6 copy-start.8
  603.5 53.9 %reduce-scatter.10.cloned.1.call-start = ((), (), s32[]{:S(2)}) async-start(), calls=%async_computation.12 | async-start | bytes 1474560 | tf_op jit(solution)/shard_map/reduce_scatter | solution.py:256
  604.1 113.2 %reduce-scatter.14.cloned.1.call-start = ((), (), s32[]{:S(2)}) async-start(), calls=%async_computation.14 | async-start | bytes 5898240 | tf_op jit(solution)/shard_map/reduce_scatter | solution.py:172
  618.5 158.6 %reduce-scatter.12.cloned.1.call-start = ((), (), s32[]{:S(2)}) async-start(), calls=%async_computation.13 | async-start | bytes 5898240 | tf_op jit(solution)/shard_map/reduce_scatter | solution.py:169
  631.0 13.6 %copy-start.24 = (f32[512]{0:T(512)S(1)}, f32[512]{0:T(512)}, u32[]{:S(2)}) copy-start(f32[512]{0:T(512)} %copy-done.23) | copy-start | bytes 6148
  631.0 13.6 %copy-start.3 = (f32[512,768]{1,0:T(8,128)S(1)}, f32[512,768]{1,0:T(8,128)}, u32[]{:S(2)}) copy-start(f32[512,768]{1,0:T(8,128)} %copy-done.2) | copy-start | bytes 4718596
  631.1 196.3 %reduce-scatter.8.cloned.1.call-start = ((), (), s32[]{:S(2)}) async-start(), calls=%async_computation.11 | async-start | bytes 4423680 | tf_op jit(solution)/shard_map/reduce_scatter | solution.py:253
  (5 other events, 5.9 us)
Sparse Core Ops, SparseCore 0:
  9.9 49.8 all-gather.4
  61.6 27.5 all-gather.6
  603.6 21.6 reduce-scatter.15
  628.7 28.6 reduce-scatter.9
  660.3 56.9 reduce-scatter.13
  720.1 56.9 reduce-scatter.11
  780.2 47.1 reduce-scatter.7
where the time goes:
time: 844 us; the launch traced here: 837 us
  waiting for transfers between devices  276 us (33%)
  blocking collectives  225 us (27%)
  matrix products  174 us (21%)
  local copies, waits for them, and re-layouts  75.8 us (9%)
  other arithmetic  49.6 us (6%)
  starting transfers between devices  18.8 us (2%)
  between operations  17.8 us (2%)
    psum x1, blocking collectives, on_device(): lax.psum((grad_qkv, grad_attn_out, grad_router, grad_gain_attn, grad_gain...  189 us
    reduce_scatter x1, waiting for transfers between devices, on_device(): lax.psum_scatter(full_w_out.astype(jnp.bfloat16), 'dp', scatter_dimension...  58 us
    reduce_scatter x1, waiting for transfers between devices, on_device(): lax.psum_scatter(full_w_in.astype(jnp.bfloat16), 'dp', scatter_dimension=...  57 us
    reduce_scatter x1, waiting for transfers between devices, on_device(): lax.psum_scatter(summed[0].astype(jnp.bfloat16), 'dp', scatter_dimension=...  47.4 us
    all_to_all x1, waiting for transfers between devices, on_device(): lax.all_to_all(send_rows, 'expert', split_axis=0, concat_axis=0, tiled=True)  29.9 us
    all_to_all x1, waiting for transfers between devices, on_device(): lax.all_to_all(d_rows, 'expert', split_axis=0, concat_axis=0, tiled=True)  28.9 us
    all_to_all x1, waiting for transfers between devices, on_device(): lax.all_to_all(d_send, 'expert', split_axis=0, concat_axis=0, tiled=True)  23.6 us
    dot_general x1, matrix products, on_device(): jnp.einsum('nekd,edf->nekf', d_recv, w_out, preferred_element_type=jnp.fl...  22 us
  transfers between devices with their start and end apart: 11, of which 9 were waited for; matrix products, arithmetic and copies ran while one was open for 25% of the time, Pallas kernels for 0%

commit v1 on v0

--- a/solution.py
+++ b/solution.py
@@ -5,6 +5,29 @@
 
 norm_eps = 1e-06
 rel_edges = (19, 21, 24, 27, 31, 35, 40, 46, 52, 59, 67, 77, 87, 99, 113)
+
+
+def split_up(x, dim, size):
+    shape = x.shape
+    tiles = x.reshape(*shape[:dim], size, shape[dim] // size, *shape[dim + 1 :])
+    return jnp.moveaxis(tiles, dim, 0)
+
+
+def joined_along(pieces, dim):
+    pieces = jnp.moveaxis(pieces, 0, dim)
+    lengths = pieces.shape
+    return pieces.reshape(*lengths[:dim], lengths[dim] * lengths[dim + 1], *lengths[dim + 2 :])
+
+
+def swapped_with_each(x, axis, split_dim, concat_dim):
+    size, index = (lax.axis_size(axis), lax.axis_index(axis))
+    blocks = split_up(x, split_dim, size)
+    done = [blocks[index]]
+    for step in range(1, size):
+        sent = blocks[index ^ step]
+        done.append(lax.ppermute(sent, axis, [(i, i ^ step) for i in range(size)]))
+    blocks = jnp.stack(done)[index ^ jnp.arange(size)]
+    return joined_along(blocks, concat_dim)
 
 
 def rms_apply(vector, gain_vec):
@@ -164,7 +187,7 @@
     d_rows = jnp.einsum("nekf,edf->nekd", d_pre, w_in, preferred_element_type=jnp.float32).astype(
         jnp.bfloat16
     )
-    d_returned = lax.all_to_all(d_rows, "expert", split_axis=0, concat_axis=0, tiled=True)
+    d_returned = swapped_with_each(d_rows, "expert", 0, 0)
     grad_w_in, grad_w_out = (
         lax.psum_scatter(
             full_w_in.astype(jnp.bfloat16), "dp", scatter_dimension=2, tiled=True

time: 844 us -> 876 us (1.038)
  waiting for transfers between devices: 276 us -> 286 us
  local copies, waits for them, and re-layouts: 75.8 us -> 85.6 us
    ppermute x0 -> x7, waiting for transfers between devices: none -> 57.1 us  [swapped_with_each(): done.append(lax.ppermute(sent, axis, [(i, i ^ step) for i in range(size)]))]
    all_to_all x1 -> x0, waiting for transfers between devices: 28.9 us -> none  [on_device(): lax.all_to_all(d_rows, 'expert', split_axis=0, concat_axis=0, tiled=True)]
    all_to_all x1, waiting for transfers between devices: 17.9 us -> 0.01 us  [on_device(): lax.all_to_all(expert_out, 'expert', split_axis=0, concat_axis=0, tiled=T...]
    ppermute x0 -> x7, starting transfers between devices: none -> 9.2 us  [swapped_with_each(): done.append(lax.ppermute(sent, axis, [(i, i ^ step) for i in range(size)]))]
  transfers between devices with their start and end apart: 11 -> 17, of which waited for: 9 -> 10; matrix products, arithmetic and copies ran while one was open for 25% -> 25% of each run, Pallas kernels for 0% -> 0%
where the time goes in v1:
time: 876 us; the launch traced here: 868 us
  waiting for transfers between devices  286 us (33%)
  blocking collectives  225 us (26%)
  matrix products  179 us (20%)
  local copies, waits for them, and re-layouts  85.6 us (10%)
  other arithmetic  51.1 us (6%)
  starting transfers between devices  23.1 us (3%)
  between operations  18 us (2%)
    psum x1, blocking collectives, on_device(): lax.psum((grad_qkv, grad_attn_out, grad_router, grad_gain_attn, grad_gain...  189 us
    reduce_scatter x1, waiting for transfers between devices, on_device(): lax.psum_scatter(full_w_out.astype(jnp.bfloat16), 'dp', scatter_dimension...  58 us
    ppermute x7, waiting for transfers between devices, swapped_with_each(): done.append(lax.ppermute(sent, axis, [(i, i ^ step) for i in range(size)]))  57.1 us
    reduce_scatter x1, waiting for transfers between devices, on_device(): lax.psum_scatter(full_w_in.astype(jnp.bfloat16), 'dp', scatter_dimension=...  57 us
    reduce_scatter x1, waiting for transfers between devices, on_device(): lax.psum_scatter(summed[0].astype(jnp.bfloat16), 'dp', scatter_dimension=...  47.4 us
    all_to_all x1, waiting for transfers between devices, on_device(): lax.all_to_all(send_rows, 'expert', split_axis=0, concat_axis=0, tiled=True)  30 us
    all_to_all x1, waiting for transfers between devices, on_device(): lax.all_to_all(d_send, 'expert', split_axis=0, concat_axis=0, tiled=True)  23.6 us
    dot_general x1, matrix products, on_device(): jnp.einsum('nekd,edf->nekf', d_recv, w_out, preferred_element_type=jnp.fl...  22.2 us
  transfers between devices with their start and end apart: 17, of which 10 were waited for; matrix products, arithmetic and copies ran while one was open for 25% of the time, Pallas kernels for 0%

profile of v1, /device:TPU:0, one launch (start us, length us, event | category | flops | bytes accessed | tf_op | source)
XLA Modules:
  0.0 868.0 jit_solution(8608930864037233032)
XLA Ops:
  14.5 11.6 %all-reduce.9 = (bf16[768]{0:T(1024)(128)(2,1)S(1)}, bf16[768]{0:T(1024)(128)(2,1)S(1)}) all-reduce(bf16[768]{0:T(1024)(128)(2,1)S(1)} %dynamic-update-slice, bf16[768]{0:T(1024)(128)(2,1)S(1)} %dynamic-update-slice.1), channel_id=1, replica_groups=mesh['dp'=4,'expert'=8] {'dp'}, use_global_device_ids=true, to_apply=%add.2 | all-reduce | flops 1536 | bytes 6144
  26.0 7.3 all-gather
  37.0 7.6 scatter_custom_fusion.1
  44.7 4.5 scatter_custom_fusion
  49.3 8.5 fusion.1
  59.8 4.1 convolution_convert_fusion
  66.9 15.8 %fusion.134 = (f32[12,512]{1,0:T(8,128)S(1)}, f32[12,512,512]{1,2,0:T(8,128)S(1)}) fusion(f32[512,512,12]{0,2,1:T(8,128)} %fusion.1, bf16[512,12,64]{0,2,1:T(8,128)(2,1)S(1)} %bitcast.277, bf16[512,12,64]{0,2,1:T(8,128)(2,1)S(1)} %bitcast.271, pred[512,512]{0,1:T(8,128)(4,1)S(1)} %fusion.94), kind=kOutput, calls=%fused_computation.211 | convolution fusion | flops 415229952 | bytes 27025408 | tf_op jit(solution)/shard_map/while/body/eval_jaxpr/qhd,khd->hqk/dot_general | solution.py:103
  87.6 7.1 fusion.73
  98.7 5.0 gather_fusion
  105.3 4.8 all-to-all-start
  110.1 8.1 all-gather.1
  118.6 5.5 gather_fusion.2
  124.9 5.9 gather_fusion.3
  130.8 4.1 multiply_convert_fusion.1
  134.9 30.0 %all-to-all-done = bf16[8,1,192,768]{3,2,1,0:T(8,128)(2,1)} async-done(((bf16[8,1,192,768]{3,2,1,0:T(8,128)(2,1)}), bf16[8,1,192,768]{3,2,1,0:T(8,128)(2,1)}, u32[]{:S(2)}, u32[]{:S(2)}) %all-to-all-start) | async-done | bytes 2359328 | tf_op jit(solution)/shard_map/all_to_all | solution.py:146
  164.9 4.5 all-to-all-start.2
  169.4 13.8 %fusion.38 = f32[8,192,3072]{2,1,0:T(8,128)} fusion(bf16[1,768,3072]{2,1,0:T(8,128)(2,1)} %param.22, bf16[8,1,192,768]{3,2,1,0:T(8,128)(2,1)} %all-to-all-done), kind=kOutput, calls=%fused_computation.55 | convolution fusion | flops 7247757312 | bytes 25952256 | tf_op jit(solution)/shard_map/nekd,edf->nekf/dot_general | solution.py:147
  183.2 17.3 %convert_bitcast_fusion = bf16[8,1,192,768]{3,2,1,0:T(8,128)(2,1)} fusion(bf16[1,768,3072]{2,1,0:T(8,128)(2,1)} %param.23, f32[8,192,3072]{2,1,0:T(8,128)} %fusion.38), kind=kOutput, calls=%fused_computation.76 | convolution fusion | flops 7291404288 | bytes 25952256 | tf_op jit(solution)/shard_map/nekf,edf->nekd/dot_general | solution.py:149
  200.4 23.6 %all-to-all-done.2 = bf16[8,1,192,768]{3,2,1,0:T(8,128)(2,1)} async-done(((bf16[8,1,192,768]{3,2,1,0:T(8,128)(2,1)}), bf16[8,1,192,768]{3,2,1,0:T(8,128)(2,1)}, u32[]{:S(2)}, u32[]{:S(2)}) %all-to-all-start.2) | async-done | bytes 2359328 | tf_op jit(solution)/shard_map/all_to_all | solution.py:177
  224.0 4.4 all-to-all-start.1
  228.5 22.2 %fusion.8 = bf16[8,1,192,3072]{3,2,0,1:T(8,128)(2,1)S(1)} fusion(f32[8,192,3072]{2,1,0:T(8,128)} %fusion.38, bf16[1,768,3072]{2,1,0:T(8,128)(2,1)} %param.23, bf16[8,1,192,768]{3,2,1,0:T(8,128)(2,1)} %all-to-all-done.2), kind=kOutput, calls=%fused_computation.19 | convolution fusion | flops 7342129152 | bytes 35389440 | tf_op jit(solution)/shard_map/nekd,edf->nekf/dot_general | solution.py:181
  250.7 13.5 %fusion.56 = bf16[8,192,768]{2,1,0:T(8,128)(2,1)S(1)} fusion(bf16[1,768,3072]{2,1,0:T(8,128)(2,1)} %param.22, bf16[8,1,192,3072]{3,2,0,1:T(8,128)(2,1)S(1)} %fusion.8), kind=kOutput, calls=%fused_computation.77 | convolution fusion | flops 7248936960 | bytes 16515072 | tf_op jit(solution)/shard_map/nekf,edf->nekd/dot_general | solution.py:187
  274.2 17.1 %collective-permute-done.1 = bf16[1,1,192,768]{3,2,1,0:T(8,128)(2,1)S(1)} collective-permute-done((bf16[1,1,192,768]{3,2,1,0:T(8,128)(2,1)S(1)}, bf16[1,1,192,768]{3,2,1,0:T(8,128)(2,1)S(1)}, u32[]{:S(2)}, u32[]{:S(2)}) %collective-permute-start.1) | collective-permute-done | bytes 294944 | tf_op jit(solution)/shard_map/ppermute | solution.py:28
  292.9 6.4 collective-permute-done.2
  300.0 33.6 %collective-permute-done.3 = bf16[1,1,192,768]{3,2,1,0:T(8,128)(2,1)S(1)} collective-permute-done((bf16[1,1,192,768]{3,2,1,0:T(8,128)(2,1)S(1)}, bf16[1,1,192,768]{3,2,1,0:T(8,128)(2,1)S(1)}, u32[]{:S(2)}, u32[]{:S(2)}) %collective-permute-start.3) | collective-permute-done | bytes 294944 | tf_op jit(solution)/shard_map/ppermute | solution.py:28
  336.6 3.8 gather_fusion.4
  343.6 7.5 gather_fusion.5
  351.1 5.3 reshape.583
  356.4 6.8 reduce_sum.183
  363.2 3.3 concatenate.10
  366.4 7.5 gather_fusion.1
  374.0 4.9 reshape.582
  378.9 9.6 %multiply_reduce_fusion.1 = (f32[512,2]{1,0:T(8,128)}, f32[512,768]{1,0:T(8,128)}) fusion(f32[512,2,768]{2,1,0:T(2,128)} %reshape.582, f32[512,768]{1,0:T(8,128)S(1)} %convert_multiply_fusion.4, f32[512,2]{1,0:T(8,128)S(1)} %copy.124), kind=kLoop, calls=%fused_computation.61 | loop fusion | flops 2751488 | bytes 6299648 | tf_op jit(solution)/shard_map/reduce_sum | solution.py:167
  398.5 7.7 fusion.70
  406.2 7.7 multiply_reduce_fusion
  413.9 5.4 multiply_convert_fusion
  419.4 10.4 %fusion.74 = f32[12,32]{1,0:T(8,128)S(1)} fusion(s32[512,512]{0,1:T(8,128)} %copy-done.12, bf16[12,512,512]{1,2,0:T(8,128)(2,1)} %multiply_convert_fusion), kind=kOutput, calls=%fused_computation.101 | convolution fusion | flops 209715200 | bytes 7341568 | tf_op jit(solution)/shard_map/while/body/eval_jaxpr/hqk,qkb->hb/dot_general | solution.py:244
  429.7 4.9 multiply_convert_fusion.2
  436.1 5.2 fusion.95
  441.3 3.7 fusion.64
  444.9 188.6 %all-reduce.11 = (bf16[768,2304]{1,0:T(8,128)(2,1)}, bf16[768,768]{1,0:T(8,128)(2,1)}, bf16[768,8]{0,1:T(8,128)(2,1)S(1)}, bf16[768]{0:T(1024)(128)(2,1)S(1)}, b...) all-reduce(f32[768,2304]{1,0:T(8,128)} %fusion.95, ...), channel_id=1, replica_groups=mesh['dp'=4,'expert'=8] {'expert'}, use_global_device_ids=true, to_apply=%region_20.21 | all-reduce | flops 2367360 | bytes 14204160 | tf_op jit(solution)/shard_map/psum | solution.py:271
  635.0 14.4 %fusion.43 = bf16[1,768,3072]{2,1,0:T(8,128)(2,1)} fusion(f32[8,192,3072]{2,1,0:T(8,128)} %fusion.38, bf16[8,1,192,768]{3,2,1,0:T(8,128)(2,1)} %all-to-all-done.2), kind=kOutput, calls=%fused_computation.59 | convolution fusion | flops 7292583936 | bytes 25952256 | tf_op jit(solution)/shard_map/nekd,nekf->edf/dot_general | solution.py:183
  649.5 12.4 %fusion.40 = bf16[1,768,3072]{2,1,0:T(8,128)(2,1)} fusion(bf16[8,1,192,3072]{3,2,0,1:T(8,128)(2,1)} %copy-done.35, bf16[8,1,192,768]{3,2,1,0:T(8,128)(2,1)} %all-to-all-done), kind=kOutput, calls=%fused_computation.58 | convolution fusion | flops 7250116608 | bytes 16515072 | tf_op jit(solution)/shard_map/nekd,nekf->edf/dot_general | solution.py:186
  664.0 9.7 %all-reduce.8 = (bf16[768]{0:T(1024)(128)(2,1)S(1)}, bf16[768]{0:T(1024)(128)(2,1)S(1)}, bf16[12,32]{1,0:T(8,128)(2,1)S(1)}) all-reduce(bf16[768]{0:T(1024)(128)(2,1)S(1)} %get-tuple-element.77, bf16[768]{0:T(1024)(128)(2,1)S(1)} %get-tuple-element.78, ...), channel_id=5, replica_groups=mesh['dp'=4,'expert'=8] {'dp'}, use_global_device_ids=true, to_apply=%region_28.29.clone | all-reduce | flops 1920 | bytes 7680
  679.8 8.5 reduce-scatter.10.cloned.1.call-done
  690.1 58.0 %reduce-scatter.14.cloned.1.call-done = bf16[1,768,768]{2,1,0:T(8,128)(2,1)} async-done(((bf16[1,768,3072]{2,1,0:T(8,128)(2,1)}), bf16[1,768,768]{2,1,0:T(8,128)(2,1)}) %reduce-scatter.14.cloned.1.call-update) | async-done | bytes 1179664 | tf_op jit(solution)/shard_map/reduce_scatter | solution.py:195
  751.0 57.0 %reduce-scatter.12.cloned.1.call-done = bf16[1,768,768]{2,1,0:T(8,128)(2,1)} async-done(((bf16[1,768,3072]{2,1,0:T(8,128)(2,1)}), bf16[1,768,768]{2,1,0:T(8,128)(2,1)}) %reduce-scatter.12.cloned.1.call-update) | async-done | bytes 1179664 | tf_op jit(solution)/shard_map/reduce_scatter | solution.py:192
  810.8 47.4 %reduce-scatter.8.cloned.1.call-done = bf16[192,2304]{1,0:T(8,128)(2,1)} async-done(((bf16[768,2304]{1,0:T(8,128)(2,1)}), bf16[192,2304]{1,0:T(8,128)(2,1)}) %reduce-scatter.8.cloned.1.call-update) | async-done | bytes 884752 | tf_op jit(solution)/shard_map/reduce_scatter | solution.py:276
  (208 shorter events, 74.3 us)
Async XLA Ops:
  7.2 5.5 copy-start.29
  7.2 5.2 copy-start.15
  7.2 6.8 copy-start.33
  7.2 7.0 copy-start.34
  7.2 18.8 %copy-start.30 = (bf16[3,32]{1,0:T(4,128)(2,1)S(1)}, bf16[3,32]{1,0:T(4,128)(2,1)}, u32[]{:S(2)}) copy-start(bf16[3,32]{1,0:T(4,128)(2,1)} %param.21) | copy-start | bytes 580
  7.2 52.6 %all-gather.5.cloned.1.call-start = ((), (), s32[]{:S(2)}) async-start(), calls=%async_computation.8 | async-start | bytes 4423680 | tf_op jit(solution)/shard_map/all_gather | solution.py:61
  8.0 86.8 %all-gather.7.cloned.1.call-start = ((), (), s32[]{:S(2)}) async-start(), calls=%async_computation.9 | async-start | bytes 1474560 | tf_op jit(solution)/shard_map/all_gather | solution.py:62
  12.4 45.4 %copy-start.12 = (s32[512,512]{0,1:T(8,128)}, s32[512,512]{0,1:T(8,128)S(1)}, u32[]{:S(2)}) copy-start(s32[512,512]{0,1:T(8,128)S(1)} %compare_select_fusion) | copy-start | bytes 3145732
  12.7 20.7 %copy-start.22 = (f32[512]{0:T(512)}, f32[512]{0:T(512)S(1)}, u32[]{:S(2)}) copy-start(f32[512]{0:T(512)S(1)} %fusion.68) | copy-start | bytes 6148
  12.7 47.1 %copy-start.26 = (f32[512]{0:T(512)}, f32[512]{0:T(512)S(1)}, u32[]{:S(2)}) copy-start(f32[512]{0:T(512)S(1)} %fusion.116) | copy-start | bytes 6148
  26.0 33.8 %copy-start.24 = (f32[768]{0:T(1024)}, f32[768]{0:T(1024)S(1)}, u32[]{:S(2)}) copy-start(f32[768]{0:T(1024)S(1)} %convert_element_type.372) | copy-start | bytes 9220
  65.2 17.5 %copy-start.6 = (bf16[512,768]{0,1:T(8,128)(2,1)}, bf16[512,768]{0,1:T(8,128)(2,1)S(1)}, u32[]{:S(2)}) copy-start(bf16[512,768]{0,1:T(8,128)(2,1)S(1)} %copy.120) | copy-start | bytes 2359300
  66.9 15.8 %copy-start.10 = (bf16[512,768]{0,1:T(8,128)(2,1)}, bf16[512,768]{0,1:T(8,128)(2,1)S(1)}, u32[]{:S(2)}) copy-start(bf16[512,768]{0,1:T(8,128)(2,1)S(1)} %copy.119) | copy-start | bytes 2359300
  82.7 4.6 copy-start
  87.6 7.2 copy-start.14
  94.8 2.5 copy-start.19
  105.3 4.8 copy-start.28
  105.3 13.0 %copy-start.17 = (bf16[512,768]{1,0:T(8,128)(2,1)S(1)}, bf16[512,768]{1,0:T(8,128)(2,1)}, u32[]{:S(2)}) copy-start(bf16[512,768]{1,0:T(8,128)(2,1)} %param.13) | copy-start | bytes 2359300
  105.3 59.5 %all-to-all-start = ((bf16[8,1,192,768]{3,2,1,0:T(8,128)(2,1)}), bf16[8,1,192,768]{3,2,1,0:T(8,128)(2,1)}, u32[]{:S(2)}, u32[]{:S(2)}) async-start(bf16[8,1,192,768]{3,2,1,0:T(8,128)(2,1)} %broadcast_multiply_fusion), calls=%async_computation | async-start | bytes 4718592 | tf_op jit(solution)/shard_map/all_to_all | solution.py:146
  118.6 5.9 copy-start.21
  164.9 59.2 %all-to-all-start.2 = ((bf16[8,1,192,768]{3,2,1,0:T(8,128)(2,1)}), bf16[8,1,192,768]{3,2,1,0:T(8,128)(2,1)}, u32[]{:S(2)}, u32[]{:S(2)}) async-start(bf16[8,1,192,768]{3,2,1,0:T(8,128)(2,1)} %multiply_convert_fusion.1), calls=%async_computation.2 | async-start | bytes 4718592 | tf_op jit(solution)/shard_map/all_to_all | solution.py:177
  224.0 139.1 %all-to-all-start.1 = ((bf16[8,1,192,768]{3,2,1,0:T(8,128)(2,1)}), bf16[8,1,192,768]{3,2,1,0:T(8,128)(2,1)}, u32[]{:S(2)}, u32[]{:S(2)}) async-start(bf16[8,1,192,768]{3,2,1,0:T(8,128)(2,1)} %convert_bitcast_fusion), calls=%async_computation.1 | async-start | bytes 4718592 | tf_op jit(solution)/shard_map/all_to_all | solution.py:152
  228.4 449.9 %reduce-scatter.16.cloned.1.call-start = ((), (), s32[]{:S(2)}) async-start(), calls=%async_computation.14 | async-start | bytes 245760
  250.7 13.5 %copy-start.35 = (bf16[8,1,192,3072]{3,2,0,1:T(8,128)(2,1)}, bf16[8,1,192,3072]{3,2,0,1:T(8,128)(2,1)S(1)}, u32[]{:S(2)}) copy-start(bf16[8,1,192,3072]{3,2,0,1:T(8,128)(2,1)S(1)} %fusion.8) | copy-start | bytes 28311556
  264.4 6.7 collective-permute-start
  264.8 26.5 %collective-permute-start.1 = (bf16[1,1,192,768]{3,2,1,0:T(8,128)(2,1)S(1)}, bf16[1,1,192,768]{3,2,1,0:T(8,128)(2,1)S(1)}, u32[]{:S(2)}, u32[]{:S(2)}) collective-permute-start(bf16[1,1,192,768]{3,2,1,0:T(8,128)(2,1)S(1)} %get-tuple-element.106), channel_id=1, source_target_pairs={{0,2},{1,3},{2,0},{3,1},{4,6},{5,7},{6,4},{7,5},{8,10},{9,11},{10,... | collective-permute-start | bytes 884744 | tf_op jit(solution)/shard_map/ppermute | solution.py:28
  267.2 68.6 %collective-permute-start.6 = (bf16[1,1,192,768]{3,2,0,1:T(8,128)(2,1)S(1)}, bf16[1,1,192,768]{3,2,0,1:T(8,128)(2,1)S(1)}, u32[]{:S(2)}, u32[]{:S(2)}) collective-permute-start(bf16[1,1,192,768]{3,2,0,1:T(8,128)(2,1)S(1)} %get-tuple-element.101), channel_id=1, source_target_pairs={{0,7},{1,6},{2,5},{3,4},{4,3},{5,2},{6,1},{7,0},{8,15},{9,14},{10,... | collective-permute-start | bytes 884744 | tf_op jit(solution)/shard_map/ppermute | solution.py:28
  269.3 65.8 %collective-permute-start.5 = (bf16[1,1,192,768]{3,2,1,0:T(8,128)(2,1)S(1)}, bf16[1,1,192,768]{3,2,1,0:T(8,128)(2,1)S(1)}, u32[]{:S(2)}, u32[]{:S(2)}) collective-permute-start(bf16[1,1,192,768]{3,2,1,0:T(8,128)(2,1)S(1)} %get-tuple-element.102), channel_id=1, source_target_pairs={{0,6},{1,7},{2,4},{3,5},{4,2},{5,3},{6,0},{7,1},{8,14},{9,15},{10,... | collective-permute-start | bytes 884744 | tf_op jit(solution)/shard_map/ppermute | solution.py:28
  270.8 63.6 %collective-permute-start.4 = (bf16[1,1,192,768]{3,2,1,0:T(8,128)(2,1)S(1)}, bf16[1,1,192,768]{3,2,1,0:T(8,128)(2,1)S(1)}, u32[]{:S(2)}, u32[]{:S(2)}) collective-permute-start(bf16[1,1,192,768]{3,2,1,0:T(8,128)(2,1)S(1)} %get-tuple-element.103), channel_id=1, source_target_pairs={{0,5},{1,4},{2,7},{3,6},{4,1},{5,0},{6,3},{7,2},{8,13},{9,12},{10,... | collective-permute-start | bytes 884744 | tf_op jit(solution)/shard_map/ppermute | solution.py:28
  271.1 28.2 %collective-permute-start.2 = (bf16[1,1,192,768]{3,2,1,0:T(8,128)(2,1)S(1)}, bf16[1,1,192,768]{3,2,1,0:T(8,128)(2,1)S(1)}, u32[]{:S(2)}, u32[]{:S(2)}) collective-permute-start(bf16[1,1,192,768]{3,2,1,0:T(8,128)(2,1)S(1)} %get-tuple-element.105), channel_id=1, source_target_pairs={{0,3},{1,2},{2,1},{3,0},{4,7},{5,6},{6,5},{7,4},{8,11},{9,10},{10,... | collective-permute-start | bytes 884744 | tf_op jit(solution)/shard_map/ppermute | solution.py:28
  291.2 42.4 %collective-permute-start.3 = (bf16[1,1,192,768]{3,2,1,0:T(8,128)(2,1)S(1)}, bf16[1,1,192,768]{3,2,1,0:T(8,128)(2,1)S(1)}, u32[]{:S(2)}, u32[]{:S(2)}) collective-permute-start(bf16[1,1,192,768]{3,2,1,0:T(8,128)(2,1)S(1)} %get-tuple-element.104), channel_id=1, source_target_pairs={{0,4},{1,5},{2,6},{3,7},{4,0},{5,1},{6,2},{7,3},{8,12},{9,13},{10,... | collective-permute-start | bytes 884744 | tf_op jit(solution)/shard_map/ppermute | solution.py:28
  389.8 2.8 copy-start.3
  389.8 2.9 copy-start.13
  394.2 2.3 copy-start.32
  398.5 15.4 %slice-start = ((s8[12582912]{0:T(1024)(128)(4,1)}), s8[4194304]{0:T(1024)(128)(4,1)S(1)}, s32[]{:S(2)}) async-start(s8[12582912]{0:T(1024)(128)(4,1)} %bitcast.268), calls=%async_computation.15 | async-start | bytes 8388608
  398.5 15.4 %slice-start.1 = ((s8[12582912]{0:T(1024)(128)(4,1)}), s8[4194304]{0:T(1024)(128)(4,1)S(1)}, s32[]{:S(2)}) async-start(s8[12582912]{0:T(1024)(128)(4,1)} %bitcast.268), calls=%async_computation.16 | async-start | bytes 8388608
  406.2 7.7 slice-start.2
  419.3 10.4 %copy-start.11 = (bf16[512,768]{0,1:T(8,128)(2,1)S(1)}, bf16[512,768]{0,1:T(8,128)(2,1)}, u32[]{:S(2)}) copy-start(bf16[512,768]{0,1:T(8,128)(2,1)} %copy-done.10) | copy-start | bytes 2359300
  429.7 5.0 copy-start.1
  429.7 5.0 copy-start.7
  436.1 5.2 copy-start.31
  441.2 3.7 copy-start.8
  634.4 53.9 %reduce-scatter.10.cloned.1.call-start = ((), (), s32[]{:S(2)}) async-start(), calls=%async_computation.11 | async-start | bytes 1474560 | tf_op jit(solution)/shard_map/reduce_scatter | solution.py:279
  634.9 113.2 %reduce-scatter.14.cloned.1.call-start = ((), (), s32[]{:S(2)}) async-start(), calls=%async_computation.13 | async-start | bytes 5898240 | tf_op jit(solution)/shard_map/reduce_scatter | solution.py:195
  649.4 158.5 %reduce-scatter.12.cloned.1.call-start = ((), (), s32[]{:S(2)}) async-start(), calls=%async_computation.12 | async-start | bytes 5898240 | tf_op jit(solution)/shard_map/reduce_scatter | solution.py:192
  661.9 13.6 %copy-start.23 = (f32[512]{0:T(512)S(1)}, f32[512]{0:T(512)}, u32[]{:S(2)}) copy-start(f32[512]{0:T(512)} %copy-done.22) | copy-start | bytes 6148
  661.9 13.6 %copy-start.5 = (f32[512,768]{1,0:T(8,128)S(1)}, f32[512,768]{1,0:T(8,128)}, u32[]{:S(2)}) copy-start(f32[512,768]{1,0:T(8,128)} %copy-done.4) | copy-start | bytes 4718596
  662.0 196.3 %reduce-scatter.8.cloned.1.call-start = ((), (), s32[]{:S(2)}) async-start(), calls=%async_computation.10 | async-start | bytes 4423680 | tf_op jit(solution)/shard_map/reduce_scatter | solution.py:276
  (8 other events, 11.1 us)
Sparse Core Ops, SparseCore 0:
  9.9 49.8 all-gather.4
  61.6 27.5 all-gather.6
  634.5 21.6 reduce-scatter.15
  659.5 28.6 reduce-scatter.9
  691.1 56.9 reduce-scatter.13
  751.0 56.9 reduce-scatter.11
  811.0 47.1 reduce-scatter.7
